TPU v7x, 32 devices: a whole 2x2x4 slice. The times are simulated.
32 devices in a mesh: lat: 8 (over z, y), chan: 4 (over x, core).
Axes of the slice: x: 2, y: 2, z: 4, core: 2. Of those that a mesh axis runs over, the one named last changes fastest.
Arguments:
- grid_in: bfloat16 [256, 384, 1024], P('chan', 'lat'), may hold values from -6 to 6
- quad_weights: float32 [384], P('lat'), may hold values from 0.5 to 2
- legendre: bfloat16 [384, 384, 384], P('lat'), as said below
- mixing: bfloat16 [2, 384, 256, 256], P(None, 'lat', 'chan'), may hold values from -0.375 to 0.375
Outputs:
- grid_out: bfloat16 [256, 384, 1024], P('chan', 'lat')
Inputs may be any that keep to these rules, and one draw needn't show every extreme that they name: legendre[m, l, t] is zero wherever l < m.
All inputs are finite; a program needn't handle non-finite values.
Results may differ from a plain program's by a relative error of at most 0.0068.
Values may be sent and summed in bfloat16 or wider, within the bound.
A program may use at most 128 MiB of HBM per device.

v0:
```python
import math
import jax
import jax.numpy as jnp
from jax import lax
from jax.sharding import PartitionSpec as P

M = 384


def fourier_table(number, length):
    orders = jnp.arange(number, dtype=jnp.int32)
    points = jnp.arange(length, dtype=jnp.int32)
    phases = orders[:, None] * points[None, :] % length
    angles = phases.astype(jnp.float32) * (2.0 * math.pi / length)
    factor = 1.0 / math.sqrt(length)
    return jnp.stack([jnp.cos(angles) * factor, -jnp.sin(angles) * factor]).astype(jnp.bfloat16)


def body(grid_in, quad_weights, legendre, mixing):
    groups = grid_in.shape[0]
    rows_lat = grid_in.shape[1]
    length = grid_in.shape[2]
    fourier = fourier_table(M, length)
    spectra = jnp.einsum("ctn,rmn->mtrc", grid_in, fourier, preferred_element_type=jnp.float32)
    spectra = spectra * quad_weights[None, :, None, None]
    weighted = spectra.astype(jnp.bfloat16).reshape(M, rows_lat, 2 * groups)
    coeffs = jnp.einsum(
        "mlt,mtk->mlk",
        legendre,
        lax.all_to_all(weighted, "lat", split_axis=0, concat_axis=1, tiled=True),
        preferred_element_type=jnp.float32,
    ).astype(jnp.bfloat16)
    by_degree = lax.all_to_all(coeffs, "lat", split_axis=1, concat_axis=0, tiled=True)
    orders = by_degree.shape[0]
    degrees = by_degree.shape[1]
    weights_out = lax.all_to_all(mixing, "chan", split_axis=3, concat_axis=2, tiled=True)
    block_in = lax.all_gather(by_degree, "chan", axis=2, tiled=True)
    shards = block_in.shape[2] // (2 * groups)
    halves = block_in.reshape(orders, degrees, shards, 2, groups)
    real_in = halves[:, :, :, 0, :].reshape(orders, degrees, shards * groups)
    imag_in = halves[:, :, :, 1, :].reshape(orders, degrees, shards * groups)
    real_weight = weights_out[0]
    imag_weight = weights_out[1]
    real_sum = jnp.einsum(
        "mlc,lcd->mld", real_in, real_weight, preferred_element_type=jnp.float32
    ) - jnp.einsum("mlc,lcd->mld", imag_in, imag_weight, preferred_element_type=jnp.float32)
    imag_sum = jnp.einsum(
        "mlc,lcd->mld", imag_in, real_weight, preferred_element_type=jnp.float32
    ) + jnp.einsum("mlc,lcd->mld", real_in, imag_weight, preferred_element_type=jnp.float32)
    mixed_coef = (
        jnp.stack([real_sum, imag_sum], axis=2)
        .reshape(orders, degrees, 2 * groups)
        .astype(jnp.bfloat16)
    )
    synthesis = jnp.einsum(
        "mlt,mlk->mtk",
        legendre,
        lax.all_to_all(mixed_coef, "lat", split_axis=0, concat_axis=1, tiled=True),
        preferred_element_type=jnp.float32,
    ).astype(jnp.bfloat16)
    gridded = lax.all_to_all(synthesis, "lat", split_axis=1, concat_axis=0, tiled=True)
    spread = gridded.reshape(M, rows_lat, 2, groups)
    restored = jnp.einsum("mtrc,rmn->ctn", spread, fourier, preferred_element_type=jnp.float32)
    return (restored + grid_in.astype(jnp.float32)).astype(jnp.bfloat16)


def solution(mesh):
    return jax.shard_map(
        body,
        mesh=mesh,
        in_specs=(
            P("chan", "lat", None),
            P("lat"),
            P("lat", None, None),
            P(None, "lat", "chan", None),
        ),
        out_specs=P("chan", "lat", None),
        check_vma=False,
    )
```

profile of v0, /device:TPU:0, one launch (start us, length us, event | category | flops | bytes accessed | tf_op | source)
XLA Modules:
  0.0 787.2 jit_solution(417036485185853445)
XLA Ops:
  6.5 6.4 multiply_convert_fusion.1
  14.1 15.9 %fusion.4 = bf16[384,48,2,64]{0,3,1,2:T(8,128)(2,1)S(1)} fusion(f32[48]{0:T(128)} %param.5, bf16[64,48,1024]{2,1,0:T(8,128)(2,1)} %param.4, bf16[1,384,1024]{2,1,0:T(8,128)(2,1)S(1)} %get-tuple-element.9, bf16[1,384,1024]{2,1,0:T(8,128)(2,1)S(1)} %get-tuple-element.10), kind=kOutput, calls=%fused_computation.7 | convolution fusion | flops 4839702528 | bytes 12583104 | tf_op jit(solution)/shard_map/ctn,rmn->mtrc/dot_general | solution.py:24
  32.8 7.0 copy.34
  39.7 111.9 %all_to_all.84 = bf16[384,48,128]{2,1,0:T(8,128)(2,1)S(1)} all-to-all(bf16[384,48,128]{2,1,0:T(8,128)(2,1)} %copy.34), channel_id=1, replica_groups=mesh['lat'=8,'chan'=4] {'lat'}, dimensions={0} | all-to-all | bytes 9437184 | tf_op jit(solution)/shard_map/all_to_all | solution.py:30
  153.0 9.2 %convert_bitcast_fusion.1 = bf16[48,384,128]{1,2,0:T(8,128)(2,1)} fusion(bf16[48,384,128]{2,1,0:T(8,128)(2,1)S(1)} %bitcast.87, bf16[48,384,384]{2,1,0:T(8,128)(2,1)} %param.6), kind=kOutput, calls=%fused_computation.12 | convolution fusion | flops 1814298624 | bytes 23592960 | tf_op jit(solution)/shard_map/mlt,mtk->mlk/dot_general | solution.py:27
  162.1 7.0 copy.37
  169.1 107.9 %all_to_all.85 = bf16[48,384,128]{2,0,1:T(8,128)(2,1)S(1)} all-to-all(bf16[48,384,128]{2,0,1:T(8,128)(2,1)} %copy.37), channel_id=1, replica_groups=mesh['lat'=8,'chan'=4] {'lat'}, dimensions={1} | all-to-all | bytes 9437184 | tf_op jit(solution)/shard_map/all_to_all | solution.py:33
  282.3 9.4 %copy.41 = bf16[2,48,64,256]{2,1,0,3:T(8,128)(2,1)} copy(bf16[2,48,64,256]{3,2,1,0:T(8,128)(2,1)S(1)} %copy-done.3) | data formatting | bytes 6291456 | tf_op args[3]
  291.7 7.2 reshape.101
  299.0 74.6 %all_to_all.86 = bf16[4,2,196608]{2,1,0:T(2,128)(2,1)} all-to-all(bf16[4,2,196608]{2,1,0:T(2,128)(2,1)S(1)} %reshape.101), channel_id=1, replica_groups=mesh['lat'=8,'chan'=4] {'chan'}, dimensions={0} | all-to-all | bytes 6291456 | tf_op jit(solution)/shard_map/all_to_all | solution.py:36
  373.5 7.5 reshape.102
  381.0 8.2 %copy.77 = bf16[2,48,64,4,64]{2,3,4,1,0:T(4,128)(2,1)S(1)} copy(bf16[2,48,64,4,64]{2,1,0,4,3:T(8,128)(2,1)} %bitcast.89) | data formatting | bytes 6291456 | tf_op jit(solution)/shard_map/all_to_all | solution.py:36
  402.4 33.2 %all-gather.2.cloned.1.call-done = bf16[384,48,512]{2,1,0:T(8,128)(2,1)} async-done(((bf16[384,48,128]{2,1,0:T(8,128)(2,1)}), bf16[384,48,512]{2,1,0:T(8,128)(2,1)}) %all-gather.2.cloned.1.call-update) | async-done | bytes 18874384 | tf_op jit(solution)/shard_map/all_gather | solution.py:37
  435.6 25.8 %copy.40 = bf16[384,48,512]{0,2,1:T(8,128)(2,1)} copy(bf16[384,48,512]{2,1,0:T(8,128)(2,1)} %all-gather.2.cloned.1.call-done) | data formatting | bytes 37748736 | tf_op jit(solution)/shard_map/all_gather | solution.py:37
  461.4 8.5 %fusion.19 = (bf16[384,48,4,1,64]{0,4,3,2,1:T(8,128)(2,1)S(1)}, bf16[384,48,4,1,64]{0,4,3,2,1:T(8,128)(2,1)S(1)}) fusion(bf16[384,48,4,2,64]{0,4,3,2,1:T(8,128)(2,1)} %bitcast.85), kind=kLoop, calls=%fused_computation.31 | loop fusion | bytes 37748736 | tf_op jit(solution)/shard_map/slice | solution.py:40
  484.4 7.0 copy.48
  491.3 110.3 %all_to_all.87 = bf16[384,48,128]{2,1,0:T(8,128)(2,1)S(1)} all-to-all(bf16[384,48,128]{2,1,0:T(8,128)(2,1)} %copy.48), channel_id=1, replica_groups=mesh['lat'=8,'chan'=4] {'lat'}, dimensions={0} | all-to-all | bytes 9437184 | tf_op jit(solution)/shard_map/all_to_all | solution.py:58
  603.0 10.5 %convert_bitcast_fusion = bf16[48,384,128]{1,2,0:T(8,128)(2,1)} fusion(bf16[48,384,128]{2,1,0:T(8,128)(2,1)S(1)} %bitcast.86, bf16[48,384,384]{2,1,0:T(8,128)(2,1)} %param.6), kind=kOutput, calls=%fused_computation.9 | convolution fusion | flops 1814298624 | bytes 23592960 | tf_op jit(solution)/shard_map/mlt,mlk->mtk/dot_general | solution.py:55
  613.5 7.0 copy.51
  620.5 108.6 %all_to_all.88 = bf16[48,384,128]{2,0,1:T(8,128)(2,1)} all-to-all(bf16[48,384,128]{2,0,1:T(8,128)(2,1)} %copy.51), channel_id=1, replica_groups=mesh['lat'=8,'chan'=4] {'lat'}, dimensions={1} | all-to-all | bytes 9437184 | tf_op jit(solution)/shard_map/all_to_all | solution.py:61
  729.1 12.4 %copy.67 = bf16[8,48,48,128]{1,0,3,2:T(8,128)(2,1)} copy(bf16[8,48,48,128]{3,1,2,0:T(8,128)(2,1)} %bitcast.97) | data formatting | bytes 9437184 | tf_op jit(solution)/shard_map/reshape | solution.py:62
  741.5 16.9 %reshape.100 = bf16[384,48,2,64]{0,3,2,1:T(8,128)(2,1)} reshape(bf16[8,48,48,128]{1,0,3,2:T(8,128)(2,1)} %copy.67) | data formatting | bytes 9437184 | tf_op jit(solution)/shard_map/reshape | solution.py:62
  758.4 15.5 %fusion = bf16[64,48,1024]{2,0,1:T(8,128)(2,1)S(1)} fusion(bf16[64,48,1024]{2,1,0:T(8,128)(2,1)} %param.4, bf16[384,48,2,64]{0,3,2,1:T(8,128)(2,1)} %reshape.100, bf16[1,384,1024]{2,1,0:T(8,128)(2,1)S(1)} %copy-done.5, bf16[1,384,1024]{2,1,0:T(8,128)(2,1)S(1)} %copy-done.7), kind=kOutput, calls=%fused_computation.1 | convolution fusion | flops 4844421120 | bytes 18874368 | tf_op jit(solution)/shard_map/mtrc,rmn->ctn/dot_general | solution.py:63
  773.9 6.2 copy.56
  (31 shorter events, 39.4 us)
Async XLA Ops:
  6.5 429.0 %all-gather.2.cloned.1.call-start = ((), (), s32[]{:S(2)}) async-start(), calls=%async_computation.5 | async-start | bytes 23592960 | tf_op jit(solution)/shard_map/all_gather | solution.py:37
  13.0 0.9 copy-start.4
  13.0 1.1 copy-start.6
  280.4 1.9 copy-start.3
  393.6 5.9 copy-start.1
  461.3 8.6 %copy-start = (bf16[48,256,64]{1,2,0:T(8,128)(2,1)S(1)}, bf16[48,256,64]{1,2,0:T(8,128)(2,1)}, u32[]{:S(2)}) copy-start(bf16[48,256,64]{1,2,0:T(8,128)(2,1)} %squeeze.6) | copy-start | bytes 4718596
  477.7 3.4 copy-start.2
  741.5 16.9 %copy-start.5 = (bf16[1,384,1024]{2,1,0:T(8,128)(2,1)S(1)}, bf16[1,384,1024]{2,1,0:T(8,128)(2,1)}, u32[]{:S(2)}) copy-start(bf16[1,384,1024]{2,1,0:T(8,128)(2,1)} %copy-done.4) | copy-start | bytes 2359300
  741.5 16.9 %copy-start.7 = (bf16[1,384,1024]{2,1,0:T(8,128)(2,1)S(1)}, bf16[1,384,1024]{2,1,0:T(8,128)(2,1)}, u32[]{:S(2)}) copy-start(bf16[1,384,1024]{2,1,0:T(8,128)(2,1)} %copy-done.6) | copy-start | bytes 2359300
Sparse Core Ops, SparseCore 0:
  280.5 154.9 all-gather.1
where the time goes:
time: 796 us; the launch traced here: 787 us
  blocking collectives  513 us (64%)
  local copies, waits for them, and re-layouts  158 us (20%)
  matrix products  62.2 us (8%)
  waiting for transfers between devices  33.2 us (4%)
  between operations  13.7 us (2%)
    all_to_all x1, blocking collectives, body(): lax.all_to_all(weighted, 'lat', split_axis=0, concat_axis=1, tiled=True)  112 us
    all_to_all x1, blocking collectives, body(): lax.all_to_all(mixed_coef, 'lat', split_axis=0, concat_axis=1, tiled=True)  110 us
    all_to_all x1, blocking collectives, body(): lax.all_to_all(synthesis, 'lat', split_axis=1, concat_axis=0, tiled=True)  109 us
    all_to_all x1, blocking collectives, body(): lax.all_to_all(coeffs, 'lat', split_axis=1, concat_axis=0, tiled=True)  108 us
    all_to_all x1, blocking collectives, body(): lax.all_to_all(mixing, 'chan', split_axis=3, concat_axis=2, tiled=True)  74.6 us
    all_gather x1, waiting for transfers between devices, body(): block_in = lax.all_gather(by_degree, 'chan', axis=2, tiled=True)  33.2 us
    reshape x2, local copies, waits for them, and re-layouts, body(): spread = gridded.reshape(M, rows_lat, 2, groups)  29.3 us
    unnamed x19, local copies, waits for them, and re-layouts  27.2 us
  transfers between devices with their start and end apart: 1, of which 1 were waited for; matrix products, arithmetic and copies ran while one was open for 6% of the time, Pallas kernels for 0%

commit v1 on v0

--- a/solution.py
+++ b/solution.py
@@ -5,6 +5,19 @@
 from jax.sharding import PartitionSpec as P
 
 M = 384
+
+
+def _keep_up_types(here_x, along_axis):
+    fan = lax.axis_size(along_axis)
+    slots = [(j0, (j0 + 1) % fan) for j0 in range(fan)]
+    then = [None] * fan
+    then[fan - 1] = here_x
+    for idx in range(fan - 2, -1, -1):
+        then[idx] = lax.ppermute(then[idx + 1], along_axis, slots)
+    side_arr = jnp.concatenate(then, 2)
+    formed = lax.axis_index(along_axis)
+    high = (formed + 1) * here_x.shape[2]
+    return jnp.roll(side_arr, high, 2)
 
 
 def fourier_table(number, length):
@@ -34,7 +47,7 @@
     orders = by_degree.shape[0]
     degrees = by_degree.shape[1]
     weights_out = lax.all_to_all(mixing, "chan", split_axis=3, concat_axis=2, tiled=True)
-    block_in = lax.all_gather(by_degree, "chan", axis=2, tiled=True)
+    block_in = _keep_up_types(by_degree, "chan")
     shards = block_in.shape[2] // (2 * groups)
     halves = block_in.reshape(orders, degrees, shards, 2, groups)
     real_in = halves[:, :, :, 0, :].reshape(orders, degrees, shards * groups)

time: 796 us -> 893 us (1.12)
  waiting for transfers between devices: 33.2 us -> 165 us
  blocking collectives: 513 us -> 435 us
  local copies, waits for them, and re-layouts: 158 us -> 209 us
  between operations: 13.7 us -> 0.43 us
    ppermute x0 -> x3, waiting for transfers between devices: none -> 107 us  [_keep_up_types(): then[idx] = lax.ppermute(then[idx + 1], along_axis, slots)]
    all_to_all x1 -> x0, blocking collectives: 74.6 us -> none  [body(): lax.all_to_all(mixing, 'chan', split_axis=3, concat_axis=2, tiled=True)]
    all_to_all x0 -> x1, waiting for transfers between devices: none -> 57.9 us  [body(): lax.all_to_all(mixing, 'chan', split_axis=3, concat_axis=2, tiled=True)]
    dynamic_slice x0 -> x2, local copies, waits for them, and re-layouts: none -> 41.1 us  [_keep_up_types(): return jnp.roll(side_arr, high, 2)]
    all_gather x1 -> x0, waiting for transfers between devices: 33.2 us -> none  [body(): block_in = lax.all_gather(by_degree, 'chan', axis=2, tiled=True)]
    unnamed x19 -> x36, local copies, waits for them, and re-layouts: 27.2 us -> 59.5 us
    all_gather x1 -> x0, local copies, waits for them, and re-layouts: 25.8 us -> none  [body(): block_in = lax.all_gather(by_degree, 'chan', axis=2, tiled=True)]
  transfers between devices with their start and end apart: 1 -> 4, of which waited for: 1 -> 3; matrix products, arithmetic and copies ran while one was open for 6% -> 5% of each run, Pallas kernels for 0% -> 0%
where the time goes in v1:
time: 893 us; the launch traced here: 883 us
  blocking collectives  435 us (49%)
  local copies, waits for them, and re-layouts  209 us (23%)
  waiting for transfers between devices  165 us (18%)
  matrix products  62.2 us (7%)
    all_to_all x1, blocking collectives, body(): lax.all_to_all(weighted, 'lat', split_axis=0, concat_axis=1, tiled=True)  112 us
    all_to_all x1, blocking collectives, body(): lax.all_to_all(synthesis, 'lat', split_axis=1, concat_axis=0, tiled=True)  109 us
    all_to_all x1, blocking collectives, body(): lax.all_to_all(coeffs, 'lat', split_axis=1, concat_axis=0, tiled=True)  108 us
    ppermute x3, waiting for transfers between devices, _keep_up_types(): then[idx] = lax.ppermute(then[idx + 1], along_axis, slots)  107 us
    all_to_all x1, blocking collectives, body(): lax.all_to_all(mixed_coef, 'lat', split_axis=0, concat_axis=1, tiled=True)  106 us
    unnamed x36, local copies, waits for them, and re-layouts  59.5 us
    all_to_all x1, waiting for transfers between devices, body(): lax.all_to_all(mixing, 'chan', split_axis=3, concat_axis=2, tiled=True)  57.9 us
    dynamic_slice x2, local copies, waits for them, and re-layouts, _keep_up_types(): return jnp.roll(side_arr, high, 2)  41.1 us
  transfers between devices with their start and end apart: 4, of which 3 were waited for; matrix products, arithmetic and copies ran while one was open for 5% of the time, Pallas kernels for 0%

profile of v1, /device:TPU:0, one launch (start us, length us, event | category | flops | bytes accessed | tf_op | source)
XLA Modules:
  0.0 883.0 jit_solution(2428479887195991987)
XLA Ops:
  0.0 6.4 multiply_convert_fusion.1
  7.6 15.9 %fusion.4 = bf16[384,48,2,64]{0,3,1,2:T(8,128)(2,1)S(1)} fusion(f32[48]{0:T(128)} %param.5, bf16[64,48,1024]{2,1,0:T(8,128)(2,1)} %param.4, bf16[1,384,1024]{2,1,0:T(8,128)(2,1)S(1)} %get-tuple-element.9, bf16[1,384,1024]{2,1,0:T(8,128)(2,1)S(1)} %get-tuple-element.10), kind=kOutput, calls=%fused_computation.7 | convolution fusion | flops 4839702528 | bytes 12583104 | tf_op jit(solution)/shard_map/ctn,rmn->mtrc/dot_general | solution.py:37
  26.2 7.0 copy.34
  33.2 111.9 %all_to_all.84 = bf16[384,48,128]{2,1,0:T(8,128)(2,1)S(1)} all-to-all(bf16[384,48,128]{2,1,0:T(8,128)(2,1)} %copy.34), channel_id=1, replica_groups=mesh['lat'=8,'chan'=4] {'lat'}, dimensions={0} | all-to-all | bytes 9437184 | tf_op jit(solution)/shard_map/all_to_all | solution.py:43
  146.5 9.2 %convert_bitcast_fusion.1 = bf16[48,384,128]{1,2,0:T(8,128)(2,1)} fusion(bf16[48,384,128]{2,1,0:T(8,128)(2,1)S(1)} %bitcast.92, bf16[48,384,384]{2,1,0:T(8,128)(2,1)} %param.6), kind=kOutput, calls=%fused_computation.12 | convolution fusion | flops 1814298624 | bytes 23592960 | tf_op jit(solution)/shard_map/mlt,mtk->mlk/dot_general | solution.py:40
  155.6 7.0 copy.37
  162.6 107.9 %all_to_all.85 = bf16[48,384,128]{2,0,1:T(8,128)(2,1)S(1)} all-to-all(bf16[48,384,128]{2,0,1:T(8,128)(2,1)} %copy.37), channel_id=1, replica_groups=mesh['lat'=8,'chan'=4] {'lat'}, dimensions={1} | all-to-all | bytes 9437184 | tf_op jit(solution)/shard_map/all_to_all | solution.py:46
  273.8 53.5 %collective-permute-done = bf16[384,48,128]{2,1,0:T(8,128)(2,1)S(1)} collective-permute-done((bf16[384,48,128]{2,1,0:T(8,128)(2,1)S(1)}, bf16[384,48,128]{2,1,0:T(8,128)(2,1)S(1)}, u32[]{:S(2)}, u32[]{:S(2)}) %collective-permute-start) | collective-permute-done | bytes 4718624 | tf_op jit(solution)/shard_map/ppermute | solution.py:16
  329.5 53.6 %collective-permute-done.1 = bf16[384,48,128]{2,1,0:T(8,128)(2,1)} collective-permute-done((bf16[384,48,128]{2,1,0:T(8,128)(2,1)S(1)}, bf16[384,48,128]{2,1,0:T(8,128)(2,1)}, u32[]{:S(2)}, u32[]{:S(2)}) %collective-permute-start.1) | collective-permute-done | bytes 4718624 | tf_op jit(solution)/shard_map/ppermute | solution.py:16
  383.2 9.4 %copy.41 = bf16[2,48,64,256]{2,1,0,3:T(8,128)(2,1)} copy(bf16[2,48,64,256]{3,2,1,0:T(8,128)(2,1)S(1)} %copy-done.4) | data formatting | bytes 6291456 | tf_op args[3]
  392.6 7.8 reshape.101
  404.3 57.9 %all-to-all-done.2 = bf16[4,2,196608]{2,1,0:T(2,128)(2,1)S(1)} async-done(((bf16[4,2,196608]{2,1,0:T(2,128)(2,1)}), bf16[4,2,196608]{2,1,0:T(2,128)(2,1)S(1)}, u32[]{:S(2)}, u32[]{:S(2)}) %all-to-all-start.2) | async-done | bytes 3145760 | tf_op jit(solution)/shard_map/all_to_all | solution.py:49
  467.5 7.6 copy.77
  526.3 16.8 %constant_dynamic-slice_fusion = bf16[384,48,512]{2,1,0:T(8,128)(2,1)} fusion(bf16[384,48,1024]{2,1,0:T(8,128)(2,1)} %constant_dynamic-update-slice_fusion, s32[]{:T(128)S(6)} %select_n.34), kind=kLoop, calls=%fused_computation.37 | loop fusion | bytes 37748740 | tf_op jit(solution)/shard_map/jit(_roll_dynamic)/dynamic_slice | solution.py:20
  543.1 24.3 %copy.40 = bf16[384,48,512]{0,2,1:T(8,128)(2,1)} copy(bf16[384,48,512]{2,1,0:T(8,128)(2,1)} %constant_dynamic-slice_fusion) | data formatting | bytes 37748736 | tf_op jit(solution)/shard_map/jit(_roll_dynamic)/dynamic_slice | solution.py:20
  567.4 8.3 fusion.19
  590.2 7.0 copy.48
  597.2 106.4 %all_to_all.86 = bf16[384,48,128]{2,1,0:T(8,128)(2,1)S(1)} all-to-all(bf16[384,48,128]{2,1,0:T(8,128)(2,1)} %copy.48), channel_id=1, replica_groups=mesh['lat'=8,'chan'=4] {'lat'}, dimensions={0} | all-to-all | bytes 9437184 | tf_op jit(solution)/shard_map/all_to_all | solution.py:71
  704.9 10.5 %convert_bitcast_fusion = bf16[48,384,128]{1,2,0:T(8,128)(2,1)} fusion(bf16[48,384,128]{2,1,0:T(8,128)(2,1)S(1)} %bitcast.91, bf16[48,384,384]{2,1,0:T(8,128)(2,1)} %param.6), kind=kOutput, calls=%fused_computation.9 | convolution fusion | flops 1814298624 | bytes 23592960 | tf_op jit(solution)/shard_map/mlt,mlk->mtk/dot_general | solution.py:68
  715.5 7.0 copy.51
  722.5 109.3 %all_to_all.87 = bf16[48,384,128]{2,0,1:T(8,128)(2,1)} all-to-all(bf16[48,384,128]{2,0,1:T(8,128)(2,1)} %copy.51), channel_id=1, replica_groups=mesh['lat'=8,'chan'=4] {'lat'}, dimensions={1} | all-to-all | bytes 9437184 | tf_op jit(solution)/shard_map/all_to_all | solution.py:74
  831.8 12.3 %copy.67 = bf16[8,48,48,128]{1,0,3,2:T(8,128)(2,1)} copy(bf16[8,48,48,128]{3,1,2,0:T(8,128)(2,1)} %bitcast.103) | data formatting | bytes 9437184 | tf_op jit(solution)/shard_map/reshape | solution.py:75
  844.1 16.9 %reshape.100 = bf16[384,48,2,64]{0,3,2,1:T(8,128)(2,1)} reshape(bf16[8,48,48,128]{1,0,3,2:T(8,128)(2,1)} %copy.67) | data formatting | bytes 9437184 | tf_op jit(solution)/shard_map/reshape | solution.py:75
  861.1 15.5 %fusion = bf16[64,48,1024]{2,0,1:T(8,128)(2,1)S(1)} fusion(bf16[64,48,1024]{2,1,0:T(8,128)(2,1)} %param.4, bf16[384,48,2,64]{0,3,2,1:T(8,128)(2,1)} %reshape.100, bf16[1,384,1024]{2,1,0:T(8,128)(2,1)S(1)} %copy-done.6, bf16[1,384,1024]{2,1,0:T(8,128)(2,1)S(1)} %copy-done.8), kind=kOutput, calls=%fused_computation.1 | convolution fusion | flops 4844421120 | bytes 18874368 | tf_op jit(solution)/shard_map/mtrc,rmn->ctn/dot_general | solution.py:76
  (56 shorter events, 93.0 us)
Async XLA Ops:
  6.5 0.9 copy-start.5
  6.5 1.1 copy-start.7
  270.5 112.7 %copy-start.4 = (bf16[2,48,64,256]{3,2,1,0:T(8,128)(2,1)S(1)}, bf16[2,48,64,256]{3,2,1,0:T(8,128)(2,1)}, u32[]{:S(2)}) copy-start(bf16[2,48,64,256]{3,2,1,0:T(8,128)(2,1)} %param.7) | copy-start | bytes 9437188
  271.7 2.1 copy-start
  273.8 53.5 %collective-permute-start = (bf16[384,48,128]{2,1,0:T(8,128)(2,1)S(1)}, bf16[384,48,128]{2,1,0:T(8,128)(2,1)S(1)}, u32[]{:S(2)}, u32[]{:S(2)}) collective-permute-start(bf16[384,48,128]{2,1,0:T(8,128)(2,1)S(1)} %bitcast.86), channel_id=1, source_target_pairs={{0,1},{1,2},{2,3},{3,0},{4,5},{5,6},{6,7},{7,4},{8,9},{9,10},{10,1... | collective-permute-start | bytes 14155784 | tf_op jit(solution)/shard_map/ppermute | solution.py:16
  327.4 2.1 copy-start.2
  329.5 53.7 %collective-permute-start.1 = (bf16[384,48,128]{2,1,0:T(8,128)(2,1)S(1)}, bf16[384,48,128]{2,1,0:T(8,128)(2,1)}, u32[]{:S(2)}, u32[]{:S(2)}) collective-permute-start(bf16[384,48,128]{2,1,0:T(8,128)(2,1)S(1)} %collective-permute-done), channel_id=1, source_target_pairs={{0,1},{1,2},{2,3},{3,0},{4,5},{5,6},{6,7},{7,4},{8,9},{9,10},{10,1... | collective-permute-start | bytes 14155784 | tf_op jit(solution)/shard_map/ppermute | solution.py:16
  383.2 108.2 %collective-permute-start.2 = (bf16[384,48,128]{2,1,0:T(8,128)(2,1)}, bf16[384,48,128]{2,1,0:T(8,128)(2,1)}, u32[]{:S(2)}, u32[]{:S(2)}) collective-permute-start(bf16[384,48,128]{2,1,0:T(8,128)(2,1)} %collective-permute-done.1), channel_id=1, source_target_pairs={{0,1},{1,2},{2,3},{3,0},{4,5},{5,6},{6,7},{7,4},{8,9},{9,10},{10,1... | collective-permute-start | bytes 14155784 | tf_op jit(solution)/shard_map/ppermute | solution.py:16
  400.4 61.8 %all-to-all-start.2 = ((bf16[4,2,196608]{2,1,0:T(2,128)(2,1)}), bf16[4,2,196608]{2,1,0:T(2,128)(2,1)S(1)}, u32[]{:S(2)}, u32[]{:S(2)}) async-start(bf16[4,2,196608]{2,1,0:T(2,128)(2,1)} %reshape.101), calls=%async_computation.2 | async-start | bytes 6291456 | tf_op jit(solution)/shard_map/all_to_all | solution.py:49
  485.2 17.4 %slice-start.2 = ((s8[4718592]{0:T(1024)(128)(4,1)}), s8[524288]{0:T(1024)(128)(4,1)S(1)}, s32[]{:S(2)}) async-start(s8[4718592]{0:T(1024)(128)(4,1)} %bitcast.96), calls=%async_computation.7 | async-start | bytes 1048576
  491.4 11.2 %slice-start.3 = ((s8[4718592]{0:T(1024)(128)(4,1)}), s8[4194304]{0:T(1024)(128)(4,1)S(1)}, s32[]{:S(2)}) async-start(s8[4718592]{0:T(1024)(128)(4,1)} %bitcast.96), calls=%async_computation.8 | async-start | bytes 8388608
  497.0 8.8 slice-start
  502.6 3.2 slice-start.1
  567.4 8.3 copy-start.1
  583.5 3.4 copy-start.3
  844.1 16.9 %copy-start.6 = (bf16[1,384,1024]{2,1,0:T(8,128)(2,1)S(1)}, bf16[1,384,1024]{2,1,0:T(8,128)(2,1)}, u32[]{:S(2)}) copy-start(bf16[1,384,1024]{2,1,0:T(8,128)(2,1)} %copy-done.5) | copy-start | bytes 2359300
  844.1 16.9 %copy-start.8 = (bf16[1,384,1024]{2,1,0:T(8,128)(2,1)S(1)}, bf16[1,384,1024]{2,1,0:T(8,128)(2,1)}, u32[]{:S(2)}) copy-start(bf16[1,384,1024]{2,1,0:T(8,128)(2,1)} %copy-done.7) | copy-start | bytes 2359300
